TPU v7x, 256 devices: a whole 4x4x8 slice. The times are simulated.
256 devices in a mesh: vpair: 16 (over x, y), rank: 16 (over z, core).
Axes of the slice: x: 4, y: 4, z: 8, core: 2. Of those that a mesh axis runs over, the one named last changes fastest.
Arguments:
- amplitudes: bfloat16 [8, 1200, 1200], P(None, 'vpair', 'rank'), may hold values from -6 to 6
- factors: bfloat16 [1200, 8192], P('vpair', 'rank'), may hold values from -0.1875 to 0.1875
- kernel: bfloat16 [8192, 8192], P('vpair', 'rank'), may hold values from -0.875 to 0.875
- other_terms: float32 [8, 1200, 1200], P(None, 'vpair'), may hold values from -6 to 6
- virt_energy: float32 [1200], replicated, may hold values from 0.2 to 4
- pair_energy: float32 [8], replicated, may hold values from -3 to -0.5
Outputs:
- residual: float32 [8, 1200, 1200], P(None, 'vpair')
- update_rms: float32 [], replicated
All inputs are finite; a program needn't handle non-finite values.
Results may differ from a plain program's by a relative error of at most 0.0035.
Values may be sent and summed in bfloat16 or wider, within the bound.
A program may use at most 192 MiB of HBM per device.

v0:
```python
import jax
import jax.numpy as jnp
from jax import lax
from jax.sharding import Mesh
from jax.sharding import PartitionSpec as P

VPAIR = ("vpair_0", "vpair_1")
epsilon = 1e-06


def sent_to_all(shard, axis):
    copies = jnp.broadcast_to(shard, (lax.axis_size(axis), *shard.shape))
    return lax.all_to_all(copies, axis, split_axis=0, concat_axis=0, tiled=True)


def in_order(tiles, dim):
    lengths = list(tiles.shape[1:])
    lengths[dim] *= tiles.shape[0]
    return jnp.moveaxis(tiles, 0, dim).reshape(lengths)


def collect(shard, axis, dim):
    tiles = sent_to_all(shard, axis)
    return in_order(tiles, dim)


def filled_up(lines, count):
    spare = -len(lines) % count
    return jnp.pad(lines, [(0, spare)] + [(0, 0)] * (lines.ndim - 1))


def total_of(shard, axis):
    lines = shard.reshape(-1, *shard.shape[1:][-1:])
    padded = filled_up(lines, lax.axis_size(axis))
    own = lax.psum_scatter(padded, axis, scatter_dimension=0, tiled=True)
    whole = lax.all_gather(own, axis, axis=0, tiled=True)
    return whole[: len(lines)].reshape(shard.shape)


def one_axis_at_a_time(shard, axes):
    for axis in axes:
        shard = lax.psum(shard, axis)
    return shard


def shards(amplitudes, factors, kernel, other_terms, virt_energy, pair_energy):
    vpair_count = lax.axis_size(VPAIR)
    pair_count = amplitudes.shape[0]
    row_block = amplitudes.shape[1]
    virt_count = row_block * vpair_count
    right_block = kernel.shape[1]
    factor_rows = collect(factors, "rank", 1)
    factor_full = lax.all_gather(factor_rows, VPAIR, axis=0, tiled=True)
    factor_cols = lax.dynamic_slice_in_dim(
        factor_full, lax.axis_index("rank") * right_block, right_block, 1
    )
    half_done = jnp.einsum(
        "ons,sh->onh",
        collect(amplitudes, "rank", 2),
        factor_cols,
        preferred_element_type=jnp.float32,
    ).astype(jnp.bfloat16)
    kernel_sub = lax.all_to_all(kernel, VPAIR, split_axis=1, concat_axis=0, tiled=True).astype(
        jnp.float32
    )
    coupled = jnp.einsum(
        "cp,icq->ipq",
        factor_full,
        lax.all_to_all(half_done, VPAIR, split_axis=2, concat_axis=1, tiled=True),
        preferred_element_type=jnp.float32,
    )
    weighted = (kernel_sub[None] * coupled).astype(jnp.bfloat16)
    ladder_half = jnp.einsum(
        "ap,ipq->iaq", factor_full, weighted, preferred_element_type=jnp.float32
    ).astype(jnp.bfloat16)
    back_half = lax.all_to_all(ladder_half, VPAIR, split_axis=1, concat_axis=2, tiled=True)
    partial_value = jnp.einsum(
        "iaq,bq->iab", back_half, factor_cols, preferred_element_type=jnp.float32
    )
    row_energy = lax.dynamic_slice_in_dim(
        virt_energy, lax.axis_index(VPAIR) * row_block, row_block, 0
    )
    ladder = total_of(partial_value, "rank")
    residual = other_terms + ladder
    denominator = (
        row_energy[None, :, None] + virt_energy[None, None, :] - pair_energy[:, None, None]
    )
    update = residual / denominator
    squares = one_axis_at_a_time(jnp.sum(update * update), VPAIR)
    update_rms = jnp.sqrt(squares / (pair_count * virt_count * virt_count) + epsilon)
    return (residual, update_rms)


def solution(mesh):
    torus = Mesh(mesh.devices.reshape(4, 4, mesh.shape["rank"]), ("vpair_0", "vpair_1", "rank"))
    return jax.shard_map(
        shards,
        mesh=torus,
        in_specs=(
            P(None, VPAIR, "rank"),
            P(VPAIR, "rank"),
            P(VPAIR, "rank"),
            P(None, VPAIR, None),
            P(),
            P(),
        ),
        out_specs=(P(None, VPAIR, None), P()),
        check_vma=False,
    )
```

profile of v0, /device:TPU:32, one launch (start us, length us, event | category | flops | bytes accessed | tf_op | source)
XLA Modules:
  0.0 428.2 jit_solution(5133619606905226404)
XLA Ops:
  8.2 40.6 %all_to_all.56 = bf16[16,75,512]{2,1,0:T(8,128)(2,1)S(1)} all-to-all(bf16[16,75,512]{2,1,0:T(8,128)(2,1)S(1)} %broadcast_in_dim.4), channel_id=1, replica_groups=mesh['vpair_0'=4,'vpair_1'=4,'rank'=16] {'rank'}, dimensions={0} | all-to-all | bytes 2457600 | tf_op jit(solution)/shard_map/all_to_all | solution.py:13
  49.5 1.7 reshape.63
  51.2 1.8 broadcast_in_dim.5
  53.0 5.0 %all-to-all-start.2 = ((bf16[16,8,75,75]{3,1,2,0:T(8,128)(2,1)}), bf16[16,8,75,75]{3,1,2,0:T(8,128)(2,1)S(1)}, u32[]{:S(2)}, u32[]{:S(2)}) async-start(bf16[16,8,75,75]{3,1,2,0:T(8,128)(2,1)} %broadcast_in_dim.5), calls=%async_computation.2 | async-start | bytes 4915200 | tf_op jit(solution)/shard_map/all_to_all | solution.py:13
  59.0 53.9 %all-to-all-done.2 = bf16[16,8,75,75]{3,1,2,0:T(8,128)(2,1)S(1)} async-done(((bf16[16,8,75,75]{3,1,2,0:T(8,128)(2,1)}), bf16[16,8,75,75]{3,1,2,0:T(8,128)(2,1)S(1)}, u32[]{:S(2)}, u32[]{:S(2)}) %all-to-all-start.2) | async-done | bytes 1440032 | tf_op jit(solution)/shard_map/all_to_all | solution.py:13
  112.9 7.0 %all-to-all-start = ((bf16[512,16,32]{0,2,1:T(8,128)(2,1)}), bf16[512,16,32]{0,2,1:T(8,128)(2,1)S(1)}, u32[]{:S(2)}, u32[]{:S(2)}) async-start(bf16[512,16,32]{0,2,1:T(8,128)(2,1)} %bitcast), calls=%async_computation | async-start | bytes 1048576 | tf_op jit(solution)/shard_map/all_to_all | solution.py:63
  119.9 1.8 copy.40
  121.7 4.2 reshape.70
  125.9 67.6 %all-gather.5.cloned.1.call-done = bf16[16,75,8192]{2,1,0:T(8,128)(2,1)} async-done(((bf16[1,75,8192]{2,1,0:T(8,128)(2,1)}), bf16[16,75,8192]{2,1,0:T(8,128)(2,1)}) %all-gather.5.cloned.1.call-update) | async-done | bytes 19660816 | tf_op jit(solution)/shard_map/all_gather | solution.py:53
  193.5 22.4 %reshape.64 = bf16[1200,8192]{1,0:T(8,128)(2,1)} reshape(bf16[16,75,8192]{2,1,0:T(8,128)(2,1)} %all-gather.5.cloned.1.call-done) | data formatting | bytes 39321600
  215.9 2.3 fusion.4
  218.2 1.5 copy.33
  219.7 5.3 %all-to-all-start.3 = ((bf16[8,75,512]{1,0,2:T(8,128)(2,1)}), bf16[8,75,512]{1,0,2:T(8,128)(2,1)S(1)}, u32[]{:S(2)}, u32[]{:S(2)}) async-start(bf16[8,75,512]{1,0,2:T(8,128)(2,1)} %copy.33), calls=%async_computation.3 | async-start | bytes 2097152 | tf_op jit(solution)/shard_map/all_to_all | solution.py:69
  225.4 22.3 %reshape.69 = bf16[1200,8192,1]{1,0,2:T(8,128)(2,1)} reshape(bf16[16,75,8192]{2,1,0:T(8,128)(2,1)} %all-gather.5.cloned.1.call-done) | data formatting | bytes 39321600
  249.8 17.8 %fusion.3 = bf16[8,1200,32]{1,2,0:T(8,128)(2,1)} fusion(bf16[1200,8192,1]{1,0,2:T(8,128)(2,1)} %reshape.69, bf16[8,1200,32]{1,2,0:T(8,128)(2,1)S(1)} %all_to_all.47, f32[8192,32]{0,1:T(8,128)S(1)} %bitcast.57), kind=kOutput, calls=%fused_computation.6 | convolution fusion | flops 10070831104 | bytes 21938176 | tf_op jit(solution)/shard_map/ap,ipq->iaq/dot_general | solution.py:73
  267.6 3.9 copy.36
  271.5 2.4 reshape.73
  273.9 18.8 %all_to_all.57 = bf16[16,2,9600]{2,1,0:T(2,128)(2,1)} all-to-all(bf16[16,2,9600]{2,1,0:T(2,128)(2,1)S(1)} %reshape.73), channel_id=1, replica_groups=mesh['vpair_0'=4,'vpair_1'=4,'rank'=16] {'vpair_0','vpair_1'}, dimensions={0} | all-to-all | bytes 1228800 | tf_op jit(solution)/shard_map/all_to_all | solution.py:76
  292.7 3.6 reshape.74
  296.3 2.8 copy.37
  299.9 2.4 fusion.6
  302.6 30.6 %fusion = f32[40,1200]{1,0:T(8,128)S(1)} fusion(f32[608,1200]{1,0:T(8,128)S(1)} %pad.4), kind=kCustom, calls=%all-reduce-scatter | all-reduce-scatter fusion | flops 768001 | bytes 3111424
  333.2 1.9 collective-permute-start
  336.4 3.5 collective-permute-done
  341.8 39.6 %all-gather.7.cloned.1.call-done = f32[16,38,1200]{2,1,0:T(8,128)} async-done(((f32[1,38,1200]{2,1,0:T(8,128)}), f32[16,38,1200]{2,1,0:T(8,128)}) %all-gather.7.cloned.1.call-update) | async-done | bytes 2918416 | tf_op jit(solution)/shard_map/all_gather | solution.py:36
  381.4 2.1 reshape.66
  383.5 1.8 slice.4
  385.4 3.9 reshape.61
  389.3 4.8 %multiply_reduce_fusion = (f32[]{:T(128)}, f32[8,75,1200]{2,1,0:T(8,128)S(1)}) fusion(f32[8]{0:T(128)S(1)} %copy-done.3, f32[75,1200]{1,0:T(8,128)} %broadcast_add_fusion, f32[8,75,1200]{2,1,0:T(8,128)} %reshape.61, f32[8,75,1200]{2,0,1:T(8,128)} %param.9), kind=kLoop, calls=%fused_computation.4 | loop fusion | flops 3599999 | bytes 9000036 | tf_op jit(solution)/shard_map/reduce_sum | solution.py:89
  394.1 11.0 %psum.14 = f32[]{:T(128)} all-reduce(f32[]{:T(128)} %get-tuple-element.8), channel_id=1, replica_groups=mesh['vpair_0'=4,'vpair_1'=4,'rank'=16] {'vpair_0'}, use_global_device_ids=true, to_apply=%region_2.3 | all-reduce | flops 1 | bytes 8 | tf_op jit(solution)/shard_map/psum | solution.py:42
  405.1 3.4 copy.39
  408.5 11.1 %psum.15 = f32[]{:T(128)} all-reduce(f32[]{:T(128)} %psum.14), channel_id=1, replica_groups=mesh['vpair_0'=4,'vpair_1'=4,'rank'=16] {'vpair_1'}, use_global_device_ids=true, to_apply=%region_3.4 | all-reduce | flops 1 | bytes 8 | tf_op jit(solution)/shard_map/psum | solution.py:42
  (31 shorter events, 8.7 us)
Async XLA Ops:
  7.2 186.3 %all-gather.5.cloned.1.call-start = ((), (), s32[]{:S(2)}) async-start(), calls=%async_computation.5 | async-start | bytes 22282240 | tf_op jit(solution)/shard_map/all_gather | solution.py:53
  48.8 2.4 copy-start.1
  51.2 6.7 %copy-start = (bf16[512,512]{1,0:T(8,128)(2,1)S(1)}, bf16[512,512]{1,0:T(8,128)(2,1)}, u32[]{:S(2)}) copy-start(bf16[512,512]{1,0:T(8,128)(2,1)} %param.8) | copy-start | bytes 1572868
  53.0 59.9 %all-to-all-start.2 = ((bf16[16,8,75,75]{3,1,2,0:T(8,128)(2,1)}), bf16[16,8,75,75]{3,1,2,0:T(8,128)(2,1)S(1)}, u32[]{:S(2)}, u32[]{:S(2)}) async-start(bf16[16,8,75,75]{3,1,2,0:T(8,128)(2,1)} %broadcast_in_dim.5), calls=%async_computation.2 | async-start | bytes 4915200 | tf_op jit(solution)/shard_map/all_to_all | solution.py:13
  112.9 106.9 %all-to-all-start = ((bf16[512,16,32]{0,2,1:T(8,128)(2,1)}), bf16[512,16,32]{0,2,1:T(8,128)(2,1)S(1)}, u32[]{:S(2)}, u32[]{:S(2)}) async-start(bf16[512,16,32]{0,2,1:T(8,128)(2,1)} %bitcast), calls=%async_computation | async-start | bytes 1048576 | tf_op jit(solution)/shard_map/all_to_all | solution.py:63
  219.7 28.1 %all-to-all-start.3 = ((bf16[8,75,512]{1,0,2:T(8,128)(2,1)}), bf16[8,75,512]{1,0,2:T(8,128)(2,1)S(1)}, u32[]{:S(2)}, u32[]{:S(2)}) async-start(bf16[8,75,512]{1,0,2:T(8,128)(2,1)} %copy.33), calls=%async_computation.3 | async-start | bytes 2097152 | tf_op jit(solution)/shard_map/all_to_all | solution.py:69
  225.0 156.4 %all-gather.7.cloned.1.call-start = ((), (), s32[]{:S(2)}) async-start(), calls=%async_computation.6 | async-start | bytes 3481600 | tf_op jit(solution)/shard_map/all_gather | solution.py:36
  302.5 32.6 %copy-start.4 = (u32[256]{0:T(256)S(1)}, u32[256]{0:T(256)}, u32[]{:S(2)}) copy-start(u32[256]{0:T(256)} %constant.40) | copy-start | bytes 3076
  302.5 38.3 %copy-start.2 = (f32[1200]{0:T(1024)S(1)}, f32[1200]{0:T(1024)}, u32[]{:S(2)}) copy-start(f32[1200]{0:T(1024)} %param.10) | copy-start | bytes 14404
  333.2 6.6 %collective-permute-start = (f32[30,1200]{1,0:T(8,128)S(1)}, f32[30,1200]{1,0:T(8,128)S(1)}, u32[]{:S(2)}, u32[]{:S(2)}) collective-permute-start(f32[30,1200]{1,0:T(8,128)S(1)} %slice.5), channel_id=1, source_target_pairs={{0,1},{1,2},{2,3},{3,4},{4,5},{5,6},{6,7},{7,8},{8,9},{9,10},{10,1... | collective-permute-start | bytes 432008
  385.3 3.9 copy-start.3
Sparse Core Ops, SparseCore 0:
  51.3 142.0 all-gather.4
  340.9 40.4 all-gather.6
where the time goes:
time: 429 us; the launch traced here: 428 us
  waiting for transfers between devices  165 us (38%)
  blocking collectives  112 us (26%)
  local copies, waits for them, and re-layouts  87.1 us (20%)
  matrix products  22.5 us (5%)
  starting transfers between devices  19.4 us (5%)
  between operations  16.7 us (4%)
  other arithmetic  5.74 us (1%)
    all_gather x1, waiting for transfers between devices, shards(): factor_full = lax.all_gather(factor_rows, VPAIR, axis=0, tiled=True)  67.6 us
    unnamed x22, local copies, waits for them, and re-layouts  60.5 us
    all_to_all x1, waiting for transfers between devices, sent_to_all(): return lax.all_to_all(copies, axis, split_axis=0, concat_axis=0, tiled=True)  53.9 us
    all_to_all x1, blocking collectives, sent_to_all(): return lax.all_to_all(copies, axis, split_axis=0, concat_axis=0, tiled=True)  40.6 us
    all_gather x1, waiting for transfers between devices, total_of(): whole = lax.all_gather(own, axis, axis=0, tiled=True)  39.6 us
    unnamed x1, blocking collectives  30.6 us
    psum x2, blocking collectives, one_axis_at_a_time(): shard = lax.psum(shard, axis)  22.1 us
    all_to_all x1, blocking collectives, shards(): lax.all_to_all(ladder_half, VPAIR, split_axis=1, concat_axis=2, tiled=True)  18.8 us
  transfers between devices with their start and end apart: 6, of which 4 were waited for; matrix products, arithmetic and copies ran while one was open for 14% of the time, Pallas kernels for 0%

commit v1 on v0

--- a/solution.py
+++ b/solution.py
@@ -6,6 +6,13 @@
 
 VPAIR = ("vpair_0", "vpair_1")
 epsilon = 1e-06
+
+
+def stacked_exchange(x, mesh_axis, split, join):
+    size = lax.axis_size(mesh_axis)
+    shards = jnp.stack(jnp.split(x, size, axis=split), axis=0)
+    shards = lax.all_to_all(shards, mesh_axis, split_axis=0, concat_axis=0)
+    return jnp.concatenate(shards, axis=join)
 
 
 def sent_to_all(shard, axis):
@@ -73,7 +80,7 @@
     ladder_half = jnp.einsum(
         "ap,ipq->iaq", factor_full, weighted, preferred_element_type=jnp.float32
     ).astype(jnp.bfloat16)
-    back_half = lax.all_to_all(ladder_half, VPAIR, split_axis=1, concat_axis=2, tiled=True)
+    back_half = stacked_exchange(ladder_half, VPAIR, 1, 2)
     partial_value = jnp.einsum(
         "iaq,bq->iab", back_half, factor_cols, preferred_element_type=jnp.float32
     )

time: 429 us -> 423 us (0.986)
  local copies, waits for them, and re-layouts: 87.1 us -> 77.2 us
    all_to_all x1, blocking collectives: 18.8 us -> 23.4 us  [stacked_exchange(): shards = lax.all_to_all(shards, mesh_axis, split_axis=0, concat_axis=0)]
    unnamed x22 -> x35, local copies, waits for them, and re-layouts: 60.5 us -> 55.9 us
where the time goes in v1:
time: 423 us; the launch traced here: 422 us
  waiting for transfers between devices  165 us (39%)
  blocking collectives  116 us (27%)
  local copies, waits for them, and re-layouts  77.2 us (18%)
  matrix products  21.8 us (5%)
  starting transfers between devices  19.4 us (5%)
  between operations  16.8 us (4%)
  other arithmetic  5.74 us (1%)
    all_gather x1, waiting for transfers between devices, shards(): factor_full = lax.all_gather(factor_rows, VPAIR, axis=0, tiled=True)  67.6 us
    unnamed x35, local copies, waits for them, and re-layouts  55.9 us
    all_to_all x1, waiting for transfers between devices, sent_to_all(): return lax.all_to_all(copies, axis, split_axis=0, concat_axis=0, tiled=True)  53.9 us
    all_to_all x1, blocking collectives, sent_to_all(): return lax.all_to_all(copies, axis, split_axis=0, concat_axis=0, tiled=True)  40.6 us
    all_gather x1, waiting for transfers between devices, total_of(): whole = lax.all_gather(own, axis, axis=0, tiled=True)  40 us
    unnamed x1, blocking collectives  30.2 us
    all_to_all x1, blocking collectives, stacked_exchange(): shards = lax.all_to_all(shards, mesh_axis, split_axis=0, concat_axis=0)  23.4 us
    psum x2, blocking collectives, one_axis_at_a_time(): shard = lax.psum(shard, axis)  22.1 us
  transfers between devices with their start and end apart: 6, of which 4 were waited for; matrix products, arithmetic and copies ran while one was open for 14% of the time, Pallas kernels for 0%

profile of v1, /device:TPU:32, one launch (start us, length us, event | category | flops | bytes accessed | tf_op | source)
XLA Modules:
  0.0 422.3 jit_solution(18273304703761659697)
XLA Ops:
  7.2 1.0 broadcast_in_dim.4
  8.2 40.6 %all_to_all.46 = bf16[16,75,512]{2,1,0:T(8,128)(2,1)S(1)} all-to-all(bf16[16,75,512]{2,1,0:T(8,128)(2,1)S(1)} %broadcast_in_dim.4), channel_id=1, replica_groups=mesh['vpair_0'=4,'vpair_1'=4,'rank'=16] {'rank'}, dimensions={0} | all-to-all | bytes 2457600 | tf_op jit(solution)/shard_map/all_to_all | solution.py:20
  49.5 1.7 reshape.68
  51.2 1.8 broadcast_in_dim.5
  53.0 5.0 %all-to-all-start.2 = ((bf16[16,8,75,75]{3,1,2,0:T(8,128)(2,1)}), bf16[16,8,75,75]{3,1,2,0:T(8,128)(2,1)S(1)}, u32[]{:S(2)}, u32[]{:S(2)}) async-start(bf16[16,8,75,75]{3,1,2,0:T(8,128)(2,1)} %broadcast_in_dim.5), calls=%async_computation.2 | async-start | bytes 4915200 | tf_op jit(solution)/shard_map/all_to_all | solution.py:20
  58.0 1.0 copy.27
  59.0 53.9 %all-to-all-done.2 = bf16[16,8,75,75]{3,1,2,0:T(8,128)(2,1)S(1)} async-done(((bf16[16,8,75,75]{3,1,2,0:T(8,128)(2,1)}), bf16[16,8,75,75]{3,1,2,0:T(8,128)(2,1)S(1)}, u32[]{:S(2)}, u32[]{:S(2)}) %all-to-all-start.2) | async-done | bytes 1440032 | tf_op jit(solution)/shard_map/all_to_all | solution.py:20
  112.9 7.0 %all-to-all-start = ((bf16[512,16,32]{0,2,1:T(8,128)(2,1)}), bf16[512,16,32]{0,2,1:T(8,128)(2,1)S(1)}, u32[]{:S(2)}, u32[]{:S(2)}) async-start(bf16[512,16,32]{0,2,1:T(8,128)(2,1)} %bitcast), calls=%async_computation | async-start | bytes 1048576 | tf_op jit(solution)/shard_map/all_to_all | solution.py:70
  119.9 1.8 copy.38
  121.7 4.2 %reshape.75 = bf16[8,75,1200]{2,1,0:T(8,128)(2,1)S(1)} reshape(bf16[8,75,16,75]{3,2,1,0:T(8,128)(2,1)} %copy.38) | data formatting | bytes 2880000 | tf_op jit(solution)/shard_map/reshape | solution.py:26
  125.9 67.6 %all-gather.5.cloned.1.call-done = bf16[16,75,8192]{2,1,0:T(8,128)(2,1)} async-done(((bf16[1,75,8192]{2,1,0:T(8,128)(2,1)}), bf16[16,75,8192]{2,1,0:T(8,128)(2,1)}) %all-gather.5.cloned.1.call-update) | async-done | bytes 19660816 | tf_op jit(solution)/shard_map/all_gather | solution.py:60
  193.5 22.4 %reshape.69 = bf16[1200,8192]{1,0:T(8,128)(2,1)} reshape(bf16[16,75,8192]{2,1,0:T(8,128)(2,1)} %all-gather.5.cloned.1.call-done) | data formatting | bytes 39321600
  215.9 2.3 fusion.4
  218.2 1.5 copy.32
  219.7 5.3 %all-to-all-start.3 = ((bf16[8,75,512]{1,0,2:T(8,128)(2,1)}), bf16[8,75,512]{1,0,2:T(8,128)(2,1)S(1)}, u32[]{:S(2)}, u32[]{:S(2)}) async-start(bf16[8,75,512]{1,0,2:T(8,128)(2,1)} %copy.32), calls=%async_computation.3 | async-start | bytes 2097152 | tf_op jit(solution)/shard_map/all_to_all | solution.py:76
  225.4 22.3 %reshape.74 = bf16[1200,8192,1]{1,0,2:T(8,128)(2,1)} reshape(bf16[16,75,8192]{2,1,0:T(8,128)(2,1)} %all-gather.5.cloned.1.call-done) | data formatting | bytes 39321600
  248.5 2.2 all_to_all.39
  250.6 17.1 %fusion.3 = bf16[8,1200,32]{1,2,0:T(8,128)(2,1)S(1)} fusion(bf16[1200,8192,1]{1,0,2:T(8,128)(2,1)} %reshape.74, bf16[8,1200,32]{1,2,0:T(8,128)(2,1)} %all_to_all.39, f32[8192,32]{0,1:T(8,128)S(1)} %bitcast.116), kind=kOutput, calls=%fused_computation.6 | convolution fusion | flops 10070831104 | bytes 21938176 | tf_op jit(solution)/shard_map/ap,ipq->iaq/dot_general | solution.py:80
  269.3 23.4 %all_to_all.47 = bf16[16,8,75,32]{2,3,1,0:T(8,128)(2,1)S(1)} all-to-all(bf16[16,8,75,32]{2,3,1,0:T(8,128)(2,1)S(1)} %fusion.9), channel_id=1, replica_groups=mesh['vpair_0'=4,'vpair_1'=4,'rank'=16] {'vpair_0','vpair_1'}, dimensions={0} | all-to-all | bytes 1228800 | tf_op jit(solution)/shard_map/all_to_all | solution.py:14
  294.0 2.4 fusion.6
  296.6 30.2 %fusion = f32[40,1200]{1,0:T(8,128)S(1)} fusion(f32[608,1200]{1,0:T(8,128)S(1)} %pad.4), kind=kCustom, calls=%all-reduce-scatter | all-reduce-scatter fusion | flops 768001 | bytes 3111424
  326.9 1.9 collective-permute-start
  330.1 3.5 collective-permute-done
  334.6 0.9 broadcast_add_fusion
  335.4 40.0 %all-gather.7.cloned.1.call-done = f32[16,38,1200]{2,1,0:T(8,128)} async-done(((f32[1,38,1200]{2,1,0:T(8,128)}), f32[16,38,1200]{2,1,0:T(8,128)}) %all-gather.7.cloned.1.call-update) | async-done | bytes 2918416 | tf_op jit(solution)/shard_map/all_gather | solution.py:43
  375.4 2.1 reshape.71
  377.5 1.8 slice.4
  379.4 3.9 reshape.66
  383.3 4.8 %multiply_reduce_fusion = (f32[]{:T(128)}, f32[8,75,1200]{2,1,0:T(8,128)S(1)}) fusion(f32[8]{0:T(128)S(1)} %copy-done.3, f32[75,1200]{1,0:T(8,128)} %broadcast_add_fusion, f32[8,75,1200]{2,1,0:T(8,128)} %reshape.66, f32[8,75,1200]{2,0,1:T(8,128)} %param.9), kind=kLoop, calls=%fused_computation.4 | loop fusion | flops 3599999 | bytes 9000036 | tf_op jit(solution)/shard_map/reduce_sum | solution.py:96
  388.1 11.0 %psum.14 = f32[]{:T(128)} all-reduce(f32[]{:T(128)} %get-tuple-element.8), channel_id=1, replica_groups=mesh['vpair_0'=4,'vpair_1'=4,'rank'=16] {'vpair_0'}, use_global_device_ids=true, to_apply=%region_2.3 | all-reduce | flops 1 | bytes 8 | tf_op jit(solution)/shard_map/psum | solution.py:49
  399.1 3.4 copy.37
  402.5 11.1 %psum.15 = f32[]{:T(128)} all-reduce(f32[]{:T(128)} %psum.14), channel_id=1, replica_groups=mesh['vpair_0'=4,'vpair_1'=4,'rank'=16] {'vpair_1'}, use_global_device_ids=true, to_apply=%region_3.4 | all-reduce | flops 1 | bytes 8 | tf_op jit(solution)/shard_map/psum | solution.py:49
  (44 shorter events, 6.5 us)
Async XLA Ops:
  7.2 186.3 %all-gather.5.cloned.1.call-start = ((), (), s32[]{:S(2)}) async-start(), calls=%async_computation.5 | async-start | bytes 22282240 | tf_op jit(solution)/shard_map/all_gather | solution.py:60
  48.8 2.4 copy-start.1
  51.2 6.7 %copy-start = (bf16[512,512]{1,0:T(8,128)(2,1)S(1)}, bf16[512,512]{1,0:T(8,128)(2,1)}, u32[]{:S(2)}) copy-start(bf16[512,512]{1,0:T(8,128)(2,1)} %param.8) | copy-start | bytes 1572868
  53.0 59.9 %all-to-all-start.2 = ((bf16[16,8,75,75]{3,1,2,0:T(8,128)(2,1)}), bf16[16,8,75,75]{3,1,2,0:T(8,128)(2,1)S(1)}, u32[]{:S(2)}, u32[]{:S(2)}) async-start(bf16[16,8,75,75]{3,1,2,0:T(8,128)(2,1)} %broadcast_in_dim.5), calls=%async_computation.2 | async-start | bytes 4915200 | tf_op jit(solution)/shard_map/all_to_all | solution.py:20
  112.9 106.9 %all-to-all-start = ((bf16[512,16,32]{0,2,1:T(8,128)(2,1)}), bf16[512,16,32]{0,2,1:T(8,128)(2,1)S(1)}, u32[]{:S(2)}, u32[]{:S(2)}) async-start(bf16[512,16,32]{0,2,1:T(8,128)(2,1)} %bitcast), calls=%async_computation | async-start | bytes 1048576 | tf_op jit(solution)/shard_map/all_to_all | solution.py:70
  219.7 28.1 %all-to-all-start.3 = ((bf16[8,75,512]{1,0,2:T(8,128)(2,1)}), bf16[8,75,512]{1,0,2:T(8,128)(2,1)S(1)}, u32[]{:S(2)}, u32[]{:S(2)}) async-start(bf16[8,75,512]{1,0,2:T(8,128)(2,1)} %copy.32), calls=%async_computation.3 | async-start | bytes 2097152 | tf_op jit(solution)/shard_map/all_to_all | solution.py:76
  225.0 150.4 %all-gather.7.cloned.1.call-start = ((), (), s32[]{:S(2)}) async-start(), calls=%async_computation.6 | async-start | bytes 3481600 | tf_op jit(solution)/shard_map/all_gather | solution.py:43
  296.6 32.2 %copy-start.4 = (u32[256]{0:T(256)S(1)}, u32[256]{0:T(256)}, u32[]{:S(2)}) copy-start(u32[256]{0:T(256)} %constant.40) | copy-start | bytes 3076
  296.6 37.9 %copy-start.2 = (f32[1200]{0:T(1024)S(1)}, f32[1200]{0:T(1024)}, u32[]{:S(2)}) copy-start(f32[1200]{0:T(1024)} %param.10) | copy-start | bytes 14404
  326.9 6.6 %collective-permute-start = (f32[30,1200]{1,0:T(8,128)S(1)}, f32[30,1200]{1,0:T(8,128)S(1)}, u32[]{:S(2)}, u32[]{:S(2)}) collective-permute-start(f32[30,1200]{1,0:T(8,128)S(1)} %slice.5), channel_id=1, source_target_pairs={{0,1},{1,2},{2,3},{3,4},{4,5},{5,6},{6,7},{7,8},{8,9},{9,10},{10,1... | collective-permute-start | bytes 432008
  379.4 3.9 copy-start.3
Sparse Core Ops, SparseCore 0:
  51.3 142.0 all-gather.4
  334.6 40.7 all-gather.6
